TPU v7x, 32 devices: a whole 2x2x4 slice. The times are simulated.
32 devices in a mesh: dp: 8 (over y, x, core), tensor: 4 (over z).
Axes of the slice: x: 2, y: 2, z: 4, core: 2. Of those that a mesh axis runs over, the one named last changes fastest.
Arguments:
- tokens: bfloat16 [8192, 1024], P(('dp', 'tensor')), may hold values from -6 to 6
- upstream: bfloat16 [8192, 1024], P(('dp', 'tensor')), may hold values from -6 to 6
- counts: int32 [128], P('dp'), may hold values from 37 to 49, as said below
- norm_gain: float32 [1024], replicated, may hold values from 0.5 to 1.5
- norm_bias: float32 [1024], replicated, may hold values from -4 to 4
- w_qkv: bfloat16 [1024, 3072], P('dp', 'tensor'), may hold values from -0.1875 to 0.1875
- w_out: bfloat16 [1024, 1024], P('tensor', 'dp'), may hold values from -0.1875 to 0.1875
Outputs:
- grad_tokens: bfloat16 [8192, 1024], P(('dp', 'tensor'))
- grad_qkv: float32 [1024, 3072], P('dp', 'tensor')
- grad_out: float32 [1024, 1024], P('tensor', 'dp')
- grad_gain: float32 [1024], replicated
- grad_bias: float32 [1024], replicated
Inputs may be any that keep to these rules, and one draw needn't show every extreme that they name: counts[i] is the number of visible tokens of image i, held in its first slots; some image has 49 in every draw.
All inputs are finite; a program needn't handle non-finite values.
Results may differ from a plain program's by a relative error of at most 0.014.
Values may be sent and summed in bfloat16 or wider, within the bound.
A program may use at most 64 MiB of HBM per device.

v0:
```python
import jax
import jax.numpy as jnp
from jax import lax
from jax.sharding import PartitionSpec as P

HEAD = 64
CAP = 64


def layer_norm(tokens, norm_gain, norm_bias):
    values = tokens.astype(jnp.float32)
    centre = jnp.mean(values, axis=-1, keepdims=True)
    shifted = values - centre
    variance = jnp.mean(shifted * shifted, axis=-1, keepdims=True)
    inverse_std = lax.rsqrt(variance + 1e-06)
    scaled = shifted * inverse_std
    normed = (scaled * norm_gain + norm_bias).astype(jnp.bfloat16)
    return (normed, scaled, inverse_std)


def on_device(tokens, upstream, counts, norm_gain, norm_bias, w_qkv, w_out):
    local_rows = tokens.shape[0]
    own_images = local_rows // CAP
    start_image = lax.axis_index("tensor") * own_images
    own_counts = lax.dynamic_slice_in_dim(counts, start_image, own_images)
    own_live = (
        (jnp.arange(CAP, dtype=jnp.int32)[None, :] < own_counts[:, None])
        .reshape(-1)
        .astype(jnp.float32)
    )
    normed, scaled, inverse_std = layer_norm(tokens, norm_gain, norm_bias)
    all_normed = lax.all_gather(normed, "tensor", axis=0, tiled=True)
    qkv_cols = lax.all_gather(w_qkv, "dp", axis=0, tiled=True)
    out_rows = lax.all_gather(w_out, "dp", axis=1, tiled=True)
    all_upstream = lax.all_gather(upstream, "tensor", axis=0, tiled=True)
    group_rows = all_normed.shape[0]
    images = group_rows // CAP
    local_heads = qkv_cols.shape[1] // (3 * HEAD)
    slot_live = jnp.arange(CAP, dtype=jnp.int32)[None, :] < counts[:, None]
    group_live = slot_live.reshape(-1).astype(jnp.bfloat16)
    masked = all_upstream * group_live[:, None]
    projected = jnp.dot(all_normed, qkv_cols, preferred_element_type=jnp.float32).astype(
        jnp.bfloat16
    )
    projected = projected.reshape(images, CAP, local_heads, 3, HEAD)
    query_rows = projected[:, :, :, 0]
    key_rows = projected[:, :, :, 1]
    value_rows = projected[:, :, :, 2]
    score_scale = 1.0 / HEAD**0.5
    scores = (
        jnp.einsum("bqhe,bkhe->bhqk", query_rows, key_rows, preferred_element_type=jnp.float32)
        * score_scale
    )
    scores = jnp.where(slot_live[:, None, None, :], scores, -1e30)
    probs = jax.nn.softmax(scores, axis=-1)
    probs_low = probs.astype(jnp.bfloat16)
    attended = jnp.einsum(
        "bhqk,bkhe->bqhe", probs_low, value_rows, preferred_element_type=jnp.float32
    )
    attended = attended.astype(jnp.bfloat16).reshape(group_rows, local_heads * HEAD)
    out_part = lax.dot_general(
        attended, masked, (((0,), (0,)), ((), ())), preferred_element_type=jnp.float32
    )
    grad_out = lax.psum_scatter(
        out_part.astype(jnp.bfloat16), "dp", scatter_dimension=1, tiled=True
    ).astype(jnp.float32)
    grad_att = lax.dot_general(
        masked, out_rows, (((1,), (1,)), ((), ())), preferred_element_type=jnp.float32
    )
    grad_att = grad_att.astype(jnp.bfloat16).reshape(images, CAP, local_heads, HEAD)
    grad_probs = jnp.einsum(
        "bqhe,bkhe->bhqk", grad_att, value_rows, preferred_element_type=jnp.float32
    )
    row_delta = jnp.sum(probs * grad_probs, axis=-1, keepdims=True)
    grad_scores = (probs * (grad_probs - row_delta) * score_scale).astype(jnp.bfloat16)
    grad_value = jnp.einsum(
        "bhqk,bqhe->bkhe", probs_low, grad_att, preferred_element_type=jnp.float32
    ).astype(jnp.bfloat16)
    grad_query = jnp.einsum(
        "bhqk,bkhe->bqhe", grad_scores, key_rows, preferred_element_type=jnp.float32
    ).astype(jnp.bfloat16)
    grad_key = jnp.einsum(
        "bhqk,bqhe->bkhe", grad_scores, query_rows, preferred_element_type=jnp.float32
    ).astype(jnp.bfloat16)
    grad_proj = jnp.stack([grad_query, grad_key, grad_value], axis=3).reshape(
        group_rows, 3 * local_heads * HEAD
    )
    qkv_part = lax.dot_general(
        all_normed, grad_proj, (((0,), (0,)), ((), ())), preferred_element_type=jnp.float32
    )
    grad_qkv = lax.psum_scatter(
        qkv_part.astype(jnp.bfloat16), "dp", scatter_dimension=0, tiled=True
    ).astype(jnp.float32)
    grad_normed = lax.psum_scatter(
        lax.dot_general(
            grad_proj, qkv_cols, (((1,), (1,)), ((), ())), preferred_element_type=jnp.float32
        ).astype(jnp.bfloat16),
        "tensor",
        scatter_dimension=0,
        tiled=True,
    ).astype(jnp.float32)
    grad_gain, grad_bias = lax.psum(
        (jnp.sum(grad_normed * scaled, axis=0), jnp.sum(grad_normed, axis=0)), ("dp", "tensor")
    )
    grad_scaled = grad_normed * norm_gain
    grad_ln = inverse_std * (
        grad_scaled
        - jnp.mean(grad_scaled, axis=-1, keepdims=True)
        - scaled * jnp.mean(grad_scaled * scaled, axis=-1, keepdims=True)
    )
    grad_tokens = (upstream.astype(jnp.float32) * own_live[:, None] + grad_ln).astype(jnp.bfloat16)
    return (grad_tokens, grad_qkv, grad_out, grad_gain, grad_bias)


def solution(mesh):
    return jax.shard_map(
        on_device,
        mesh=mesh,
        in_specs=(
            P(("dp", "tensor"), None),
            P(("dp", "tensor"), None),
            P("dp"),
            P(),
            P(),
            P("dp", "tensor"),
            P("tensor", "dp"),
        ),
        out_specs=(P(("dp", "tensor"), None), P("dp", "tensor"), P("tensor", "dp"), P(), P()),
        check_vma=False,
    )
```

profile of v0, /device:TPU:0, one launch (start us, length us, event | category | flops | bytes accessed | tf_op | source)
XLA Modules:
  0.0 332.8 jit_solution(4929097271266516613)
XLA Ops:
  7.2 0.7 all-gather.6.cloned.1.call-update
  7.9 0.0 all-gather.4.cloned.1.call-start
  8.0 1.2 convert_reduce_fusion.1
  9.2 1.3 fusion.49
  10.5 2.1 fusion.44
  12.7 0.0 all-gather.8.cloned.1.call-start
  12.7 0.7 all-gather.8.cloned.1.call-update
  13.5 0.1 iota_compare_fusion
  13.5 0.1 reshape.102
  13.6 12.6 %all_gather.15 = bf16[256,1024]{1,0:T(8,128)(2,1)S(1)} all-gather(bf16[256,128]{1,0:T(8,128)(2,1)S(1)} %copy-done.6), channel_id=1, replica_groups=mesh['dp'=8,'tensor'=4] {'dp'}, dimensions={1}, use_global_device_ids=true | all-gather | bytes 589824 | tf_op jit(solution)/shard_map/all_gather | solution.py:34
  26.2 12.7 %all-gather.6.cloned.1.call-done = bf16[1024,768]{1,0:T(8,128)(2,1)} async-done(((bf16[128,768]{1,0:T(8,128)(2,1)}), bf16[1024,768]{1,0:T(8,128)(2,1)}) %all-gather.6.cloned.1.call-update) | async-done | bytes 1572880 | tf_op jit(solution)/shard_map/all_gather | solution.py:33
  38.9 47.8 %all-gather.4.cloned.1.call-done = bf16[1024,1024]{1,0:T(8,128)(2,1)} async-done(((bf16[256,1024]{1,0:T(8,128)(2,1)}), bf16[1024,1024]{1,0:T(8,128)(2,1)}) %all-gather.4.cloned.1.call-update) | async-done | bytes 2097168 | tf_op jit(solution)/shard_map/all_gather | solution.py:32
  86.7 3.8 %convolution_convert_fusion.2 = bf16[1024,768]{1,0:T(8,128)(2,1)S(1)} fusion(bf16[1024,1024]{1,0:T(8,128)(2,1)} %all-gather.4.cloned.1.call-done, bf16[1024,768]{1,0:T(8,128)(2,1)} %all-gather.6.cloned.1.call-done), kind=kOutput, calls=%fused_computation.15 | convolution fusion | flops 1611399168 | bytes 5242880 | tf_op jit(solution)/shard_map/dot_general | solution.py:42
  90.6 5.0 %reshape.105 = bf16[16,64,4,3,64]{4,3,2,1,0:T(4,128)(2,1)} reshape(bf16[1024,768]{1,0:T(8,128)(2,1)S(1)} %convolution_convert_fusion.2) | data formatting | bytes 3145728 | tf_op jit(solution)/shard_map/reshape | solution.py:45
  95.5 11.4 %fusion.71 = (bf16[16,64,4,1,64]{4,3,2,1,0:T(2,128)(2,1)S(1)}, bf16[16,64,4,1,64]{4,3,2,1,0:T(2,128)(2,1)}, bf16[16,64,4,1,64]{4,3,2,1,0:T(2,128)(2,1)}) fusion(bf16[16,64,4,3,64]{4,3,2,1,0:T(4,128)(2,1)} %reshape.105), kind=kLoop, calls=%fused_computation.78 | loop fusion | bytes 3145728 | tf_op jit(solution)/shard_map/slice | solution.py:48
  106.9 25.9 %all-gather.8.cloned.1.call-done = bf16[1024,1024]{1,0:T(8,128)(2,1)} async-done(((bf16[256,1024]{1,0:T(8,128)(2,1)}), bf16[1024,1024]{1,0:T(8,128)(2,1)}) %all-gather.8.cloned.1.call-update) | async-done | bytes 2097168 | tf_op jit(solution)/shard_map/all_gather | solution.py:35
  132.8 3.1 fusion.33
  136.0 2.0 reshape.98
  138.0 1.4 copy.48
  139.3 2.9 fusion.62
  142.3 4.8 %fusion.72 = (f32[16,4,64]{2,1,0:T(4,128)S(1)}, f32[16,4,64,64]{2,3,1,0:T(8,128)}) fusion(pred[16,64]{1,0:T(8,128)(4,1)S(1)} %get-tuple-element.14, bf16[16,64,4,1,64]{4,3,2,1,0:T(2,128)(2,1)} %get-tuple-element.13, bf16[16,64,4,1,64]{4,3,2,1,0:T(2,128)(2,1)} %get-tuple-element.12), kind=kOutput, calls=%fused_computation.79 | convolution fusion | flops 34603072 | bytes 2114560 | tf_op jit(solution)/shard_map/sub | solution.py:55
  147.1 3.4 %fusion.25 = bf16[16,64,4,1,64]{1,4,2,0,3:T(8,128)(2,1)} fusion(bf16[16,64,4,64]{1,3,2,0:T(8,128)(2,1)S(1)} %copy-done.1, f32[16,4,64,64]{2,3,1,0:T(8,128)} %get-tuple-element.17, f32[16,4,64]{2,1,0:T(4,128)S(1)} %get-tuple-element.16), kind=kOutput, calls=%fused_computation.28 | convolution fusion | flops 34340864 | bytes 2113536 | tf_op jit(solution)/shard_map/bhqk,bqhe->bkhe/dot_general | solution.py:76
  150.5 0.5 fusion.26
  151.0 6.1 %fusion.30 = bf16[16,64,4,1,64]{1,4,2,0,3:T(8,128)(2,1)} fusion(f32[16,4,64,64]{2,3,1,0:T(8,128)} %fusion.62, bf16[16,64,4,1,64]{4,3,2,1,0:T(2,128)(2,1)} %get-tuple-element.13, f32[16,4,64,64]{2,3,1,0:T(8,128)} %get-tuple-element.17, f32[16,4,64]{2,1,0:T(4,128)S(1)} %get-tuple-element.16), kind=kOutput, calls=%fused_computation.31 | convolution fusion | flops 35655744 | bytes 3162112 | tf_op jit(solution)/shard_map/bhqk,bkhe->bqhe/dot_general | solution.py:79
  157.1 0.7 copy.53
  157.8 0.7 reshape.100
  158.5 2.5 fusion.36
  161.0 1.0 copy.61
  162.1 0.2 reduce-scatter.8.cloned.1.call-start
  162.3 5.6 %fusion.27 = bf16[16,64,4,1,64]{1,4,2,0,3:T(8,128)(2,1)} fusion(f32[16,4,64,64]{2,3,1,0:T(8,128)} %fusion.62, bf16[16,64,4,1,64]{4,3,2,1,0:T(2,128)(2,1)S(1)} %copy-done.3, f32[16,4,64,64]{2,3,1,0:T(8,128)} %get-tuple-element.17, f32[16,4,64]{2,1,0:T(4,128)S(1)} %get-tuple-element.16), kind=kOutput, calls=%fused_computation.30 | convolution fusion | flops 35655744 | bytes 3162112 | tf_op jit(solution)/shard_map/bhqk,bqhe->bkhe/dot_general | solution.py:82
  167.9 2.3 pad_maximum_fusion
  170.2 2.4 copy.50
  172.7 3.2 reshape.99
  175.9 5.2 %convolution_convert_fusion.1 = bf16[1024,768]{1,0:T(8,128)(2,1)} fusion(bf16[1024,1024]{1,0:T(8,128)(2,1)} %all-gather.4.cloned.1.call-done, bf16[1024,768]{0,1:T(8,128)(2,1)} %reshape.99), kind=kOutput, calls=%fused_computation.14 | convolution fusion | flops 1611399168 | bytes 5242880 | tf_op jit(solution)/shard_map/dot_general | solution.py:88
  181.1 0.0 reduce-scatter.6.cloned.1.call-start
  181.2 3.2 convolution_convert_fusion
  184.4 0.1 dynamic_slice.3
  184.5 0.1 fusion.63
  184.5 0.1 reshape.101
  184.6 10.5 %reduce-scatter.10.cloned.1.call-done = bf16[128,256]{1,0:T(8,128)(2,1)} async-done(((bf16[1024,256]{1,0:T(8,128)(2,1)}), bf16[128,256]{1,0:T(8,128)(2,1)}) %reduce-scatter.10.cloned.1.call-update) | async-done | bytes 65552
  195.1 0.9 copy.62
  196.1 0.7 convert_element_type.111
  196.8 39.9 %reduce-scatter.8.cloned.1.call-done = bf16[128,768]{1,0:T(8,128)(2,1)} async-done(((bf16[1024,768]{1,0:T(8,128)(2,1)}), bf16[128,768]{1,0:T(8,128)(2,1)}) %reduce-scatter.8.cloned.1.call-update) | async-done | bytes 196624 | tf_op jit(solution)/shard_map/reduce_scatter | solution.py:91
  236.7 1.7 convert_element_type.107
  238.4 44.1 %reduce-scatter.6.cloned.1.call-done = bf16[256,1024]{1,0:T(8,128)(2,1)} async-done(((bf16[1024,1024]{1,0:T(8,128)(2,1)}), bf16[256,1024]{1,0:T(8,128)(2,1)}) %reduce-scatter.6.cloned.1.call-update) | async-done | bytes 524304 | tf_op jit(solution)/shard_map/reduce_scatter | solution.py:94
  282.5 1.6 fusion.51
  284.1 39.5 %all-reduce = (f32[1024]{0:T(1024)}, f32[1024]{0:T(1024)}) all-reduce(f32[1024]{0:T(1024)S(1)} %get-tuple-element.5, f32[1024]{0:T(1024)S(1)} %get-tuple-element.8), channel_id=1, replica_groups=mesh['dp'=8,'tensor'=4] {'dp','tensor'}, use_global_device_ids=true, to_apply=%region_11.12 | all-reduce | flops 2048 | bytes 16384 | tf_op jit(solution)/shard_map/psum | solution.py:102
  323.6 2.3 fusion.48
  (31 shorter events, 0.2 us)
Async XLA Ops:
  7.2 6.3 %copy-start.8 = (s32[16]{0:T(128)S(1)}, s32[16]{0:T(128)}, u32[]{:S(2)}) copy-start(s32[16]{0:T(128)} %param.9) | copy-start | bytes 196
  7.2 6.4 %copy-start.6 = (bf16[256,128]{1,0:T(8,128)(2,1)S(1)}, bf16[256,128]{1,0:T(8,128)(2,1)}, u32[]{:S(2)}) copy-start(bf16[256,128]{1,0:T(8,128)(2,1)} %param.13) | copy-start | bytes 196612
  7.2 31.7 %all-gather.6.cloned.1.call-start = ((), (), s32[]{:S(2)}) async-start(), calls=%async_computation.4 | async-start | bytes 1769472 | tf_op jit(solution)/shard_map/all_gather | solution.py:33
  7.9 78.8 %all-gather.4.cloned.1.call-start = ((), (), s32[]{:S(2)}) async-start(), calls=%async_computation.3 | async-start | bytes 2621440 | tf_op jit(solution)/shard_map/all_gather | solution.py:32
  12.7 120.2 %all-gather.8.cloned.1.call-start = ((), (), s32[]{:S(2)}) async-start(), calls=%async_computation.5 | async-start | bytes 2621440 | tf_op jit(solution)/shard_map/all_gather | solution.py:35
  13.4 181.8 %reduce-scatter.10.cloned.1.call-start = ((), (), s32[]{:S(2)}) async-start(), calls=%async_computation.8 | async-start | bytes 589824
  142.3 4.8 %copy-start.1 = (bf16[16,64,4,64]{1,3,2,0:T(8,128)(2,1)S(1)}, bf16[16,64,4,64]{1,3,2,0:T(8,128)(2,1)}, u32[]{:S(2)}) copy-start(bf16[16,64,4,64]{1,3,2,0:T(8,128)(2,1)} %copy.48) | copy-start | bytes 1572868
  147.1 3.4 %copy-start.10 = (f32[16,4,64,64]{2,3,1,0:T(8,128)S(1)}, f32[16,4,64,64]{2,3,1,0:T(8,128)}, u32[]{:S(2)}) copy-start(f32[16,4,64,64]{2,3,1,0:T(8,128)} %get-tuple-element.17) | copy-start | bytes 3145732
  158.5 3.8 %copy-start.3 = (bf16[16,64,4,1,64]{4,3,2,1,0:T(2,128)(2,1)S(1)}, bf16[16,64,4,1,64]{4,3,2,1,0:T(2,128)(2,1)}, u32[]{:S(2)}) copy-start(bf16[16,64,4,1,64]{4,3,2,1,0:T(2,128)(2,1)} %get-tuple-element.12) | copy-start | bytes 1572868
  162.1 5.8 %copy-start.5 = (bf16[16,64,4,1,64]{1,4,2,0,3:T(8,128)(2,1)S(1)}, bf16[16,64,4,1,64]{1,4,2,0,3:T(8,128)(2,1)}, u32[]{:S(2)}) copy-start(bf16[16,64,4,1,64]{1,4,2,0,3:T(8,128)(2,1)} %fusion.25) | copy-start | bytes 1572868
  162.1 74.6 %reduce-scatter.8.cloned.1.call-start = ((), (), s32[]{:S(2)}) async-start(), calls=%async_computation.7 | async-start | bytes 1769472 | tf_op jit(solution)/shard_map/reduce_scatter | solution.py:91
  175.9 5.3 %copy-start.4 = (bf16[1024,768]{0,1:T(8,128)(2,1)S(1)}, bf16[1024,768]{0,1:T(8,128)(2,1)}, u32[]{:S(2)}) copy-start(bf16[1024,768]{0,1:T(8,128)(2,1)} %reshape.99) | copy-start | bytes 4718596
  175.9 5.3 %copy-start.9 = (bf16[1024,768]{1,0:T(8,128)(2,1)S(1)}, bf16[1024,768]{1,0:T(8,128)(2,1)}, u32[]{:S(2)}) copy-start(bf16[1024,768]{1,0:T(8,128)(2,1)} %all-gather.6.cloned.1.call-done) | copy-start | bytes 4718596
  181.1 101.4 %reduce-scatter.6.cloned.1.call-start = ((), (), s32[]{:S(2)}) async-start(), calls=%async_computation.6 | async-start | bytes 2621440 | tf_op jit(solution)/shard_map/reduce_scatter | solution.py:94
  184.3 98.2 %copy-start = (bf16[256,1024]{1,0:T(8,128)(2,1)S(1)}, bf16[256,1024]{1,0:T(8,128)(2,1)}, u32[]{:S(2)}) copy-start(bf16[256,1024]{1,0:T(8,128)(2,1)} %param.7) | copy-start | bytes 1572868
  184.4 98.2 %copy-start.7 = (f32[1024]{0:T(1024)S(1)}, f32[1024]{0:T(1024)}, u32[]{:S(2)}) copy-start(f32[1024]{0:T(1024)} %param.10) | copy-start | bytes 12292
  184.4 139.3 %copy-start.2 = (bf16[256,1024]{1,0:T(8,128)(2,1)S(1)}, bf16[256,1024]{1,0:T(8,128)(2,1)}, u32[]{:S(2)}) copy-start(bf16[256,1024]{1,0:T(8,128)(2,1)} %param.8) | copy-start | bytes 1572868
Sparse Core Ops, SparseCore 0:
  9.9 28.9 all-gather.5
  41.0 45.6 all-gather.3
  88.3 44.4 all-gather.7
  162.2 32.9 reduce-scatter.9
  198.3 38.3 reduce-scatter.7
  238.8 43.6 reduce-scatter.5
where the time goes:
time: 333 us
  waiting for transfers between devices  182 us (55%)
  blocking collectives  52.1 us (16%)
  matrix products  41.2 us (12%)
  local copies, waits for them, and re-layouts  29 us (9%)
  between operations  14.3 us (4%)
  other arithmetic  13.4 us (4%)
    all_gather x1, waiting for transfers between devices, on_device(): all_normed = lax.all_gather(normed, 'tensor', axis=0, tiled=True)  47.8 us
    reduce_scatter x1, waiting for transfers between devices, on_device(): lax.psum_scatter(lax.dot_general(grad_proj, qkv_cols, (((1,), (1,)), ((),...  44.1 us
    reduce_scatter x1, waiting for transfers between devices, on_device(): lax.psum_scatter(qkv_part.astype(jnp.bfloat16), 'dp', scatter_dimension=0...  39.9 us
    psum x1, blocking collectives, on_device(): lax.psum((jnp.sum(grad_normed * scaled, axis=0), jnp.sum(grad_normed, axi...  39.5 us
    all_gather x1, waiting for transfers between devices, on_device(): all_upstream = lax.all_gather(upstream, 'tensor', axis=0, tiled=True)  25.9 us
    all_gather x1, waiting for transfers between devices, on_device(): qkv_cols = lax.all_gather(w_qkv, 'dp', axis=0, tiled=True)  12.7 us
    all_gather x1, blocking collectives, on_device(): out_rows = lax.all_gather(w_out, 'dp', axis=1, tiled=True)  12.6 us
    unnamed x7, waiting for transfers between devices  12 us
  transfers between devices with their start and end apart: 6, of which 6 were waited for; matrix products, arithmetic and copies ran while one was open for 15% of the time, Pallas kernels for 0%

commit v1 on v0

v1 whole, which is shorter than its diff:
```python
import functools

import jax
import jax.numpy as jnp
from jax import lax
from jax.experimental import pallas as pl
from jax.experimental.pallas import tpu as pltpu
from jax.sharding import PartitionSpec as P

HEAD = 64
CAP = 64
MAXC = 49
F32 = jnp.float32
BF16 = jnp.bfloat16


def mm(a, b):
    return lax.dot_general(a, b, (((1,), (0,)), ((), ())), preferred_element_type=F32)


def mm_nt(a, b):
    return lax.dot_general(a, b, (((1,), (1,)), ((), ())), preferred_element_type=F32)


def mm_tn(a, b):
    return lax.dot_general(a, b, (((0,), (0,)), ((), ())), preferred_element_type=F32)


def image_of(index, images):
    total = jnp.zeros_like(index)
    for i in range(1, images + 1):
        total = total + jnp.where(index >= i * MAXC, 1, 0)
    return total


def packing(rows, local_rows, images):
    row = lax.broadcasted_iota(jnp.int32, (rows, 1), 0)
    image = image_of(row, images)
    source = jnp.where(image < images, image * CAP + (row - image * MAXC), -1)
    column = lax.broadcasted_iota(jnp.int32, (rows, local_rows), 1)
    return jnp.where(column == source, 1.0, 0.0).astype(BF16)


def kernel(
    n_dp, n_t,
    counts, tokens, upstream, gain, bias, wblk,
    gt_ref, gw_ref, gb_ref,
    x_all, u_all, k_all, w_all, xhat, rstd_s, gp_all, att_all, gn_send, gn_recv,
    g_send, g_recv, z_send, z_up, z_down, acc_s, fin, a_buf, b_buf, c_buf,
    xs, xr, us, ur, ks, kr, w1s, w1r, wus, wds, wzr, wgs, wgr,
    gns, gnr, ggs, ggr, gzs, gur, gdr, fs, fr, a_s, a_r, b_s, b_r, c_s, c_r,
):
    n_g = n_dp // n_t
    n_x = n_t // 2
    dp = lax.axis_index("dp")
    z = lax.axis_index("tensor")
    g = dp // n_t
    hh = dp % n_t
    xx = hh // 2
    core = hh % 2
    local_rows, width = tokens.shape
    images = local_rows // CAP
    rows = xhat.shape[0]
    wrows, cols = wblk.shape
    hw = cols // 4
    heads = hw // HEAD

    def rc(src, dst, ss, rs, dev):
        return pltpu.make_async_remote_copy(
            src_ref=src, dst_ref=dst, send_sem=ss, recv_sem=rs, device_id=dev,
            device_id_type=pl.DeviceIdType.MESH,
        )

    def member(h):
        return (g * n_t + h, z)

    def wrow(gi, b):
        return pl.ds(pl.multiple_of((gi * n_t + b) * wrows, wrows), wrows)

    def arow(j):
        return pl.ds(pl.multiple_of(j * rows, 16), rows)

    barrier = pltpu.get_barrier_semaphore()
    for i in range(1, n_t):
        pl.semaphore_signal(barrier, inc=1, device_id=member((hh + i) % n_t), device_id_type=pl.DeviceIdType.MESH)
        pl.semaphore_signal(barrier, inc=1, device_id=(dp, (z + i) % n_t), device_id_type=pl.DeviceIdType.MESH)
    for i in range(1, n_g):
        pl.semaphore_signal(
            barrier, inc=1, device_id=(((g + i) % n_g) * n_t + hh, z), device_id_type=pl.DeviceIdType.MESH
        )
    pl.semaphore_wait(barrier, 2 * (n_t - 1) + n_g - 1)

    is_root = z == hh
    go_up = jnp.logical_and(z >= hh, z < n_t - 1)
    go_down = jnp.logical_and(z <= hh, z > 0)
    next_up = (dp, (z + 1) % n_t)
    next_down = (dp, (z + n_t - 1) % n_t)

    def w_first():
        return rc(wblk, w_all.at[wrow(g, hh)], w1s, w1r.at[hh], member(z))

    @pl.when(jnp.logical_not(is_root))
    def _():
        w_first().start()

    @pl.when(is_root)
    def _():
        w_all[wrow(g, hh), :] = wblk[...]

    select = packing(rows, local_rows, images)
    row = lax.broadcasted_iota(jnp.int32, (rows, 1), 0)
    image = image_of(row, images)
    slot = row - image * MAXC
    count_of = jnp.zeros((rows, 1), jnp.int32)
    key = lax.broadcasted_iota(jnp.int32, (8, k_all.shape[2]), 1)
    key_image = image_of(key, images)
    key_slot = key - key_image * MAXC
    key_count = jnp.zeros(key.shape, jnp.int32)
    for i in range(images):
        count = counts[z * images + i]
        count_of = jnp.where(image == i, count, count_of)
        key_count = jnp.where(key_image == i, count, key_count)
    k_all[hh] = jnp.where(key_slot < key_count, key_image.astype(F32), -1.0)
    live = jnp.where(slot < count_of, 1.0, 0.0)

    partner = hh + 1 - 2 * core

    def k_copy(i):
        return rc(k_all.at[hh], k_all.at[hh], ks.at[i - 1], kr.at[hh], member((hh + i) % n_t))

    def own_copy(buf, ss, rs, i):
        dest = partner if i == 0 else ((xx + i) % n_x) * 2 + core
        return rc(buf.at[arow(hh)], buf.at[arow(hh)], ss.at[i], rs.at[hh], member(dest))

    def relay_copy(buf, ss, rs, i):
        j = ((xx + i) % n_x) * 2 + core
        return rc(buf.at[arow(j)], buf.at[arow(j)], ss.at[n_x + i - 1], rs.at[j], member(partner))

    def arrival(buf, ss, rs, j):
        return rc(buf.at[arow(j)], buf.at[arow(j)], ss.at[0], rs.at[j], member(partner))

    values = mm(select, tokens[...])
    centre = jnp.mean(values, axis=-1, keepdims=True)
    shifted = values - centre
    inverse = lax.rsqrt(jnp.mean(shifted * shifted, axis=-1, keepdims=True) + 1e-06)
    scaled = shifted * inverse
    xhat[...] = scaled
    rstd_s[...] = inverse
    x_all[arow(hh), :] = (scaled * gain[...] + bias[...]).astype(BF16)
    u_all[arow(hh), :] = (mm(select, upstream[...]) * live).astype(BF16)
    for i in range(1, n_t):
        k_copy(i).start()
    for i in range(n_x):
        own_copy(x_all, xs, xr, i).start()
    for i in range(n_x):
        own_copy(u_all, us, ur, i).start()

    def w_up(b):
        return rc(w_all.at[wrow(g, b)], w_all.at[wrow(g, b)], wus.at[b], wzr.at[b], next_up)

    def w_down(b):
        return rc(w_all.at[wrow(g, b)], w_all.at[wrow(g, b)], wds.at[b], wzr.at[b], next_down)

    def w_group(b, i):
        k = (i - 1) * n_t + b
        return rc(
            w_all.at[wrow(g, b)], w_all.at[wrow(g, b)], wgs.at[k], wgr.at[k],
            (((g + i) % n_g) * n_t + hh, z),
        )

    def w_group_arrival(b, i):
        k = (i - 1) * n_t + b
        src = w_all.at[wrow((g + n_g - i) % n_g, b)]
        return rc(src, src, wgs.at[k], wgr.at[k], (((g + i) % n_g) * n_t + hh, z))

    for b in range(n_t):
        block = w_all.at[wrow(g, b)]

        @pl.when(jnp.logical_and(is_root, hh != b))
        def _():
            rc(block, block, w1s, w1r.at[b], member(partner)).wait_recv()

        @pl.when(jnp.logical_not(is_root))
        def _():
            rc(block, block, wus.at[b], wzr.at[b], next_up).wait_recv()

        @pl.when(go_up)
        def _():
            w_up(b).start()

        @pl.when(go_down)
        def _():
            w_down(b).start()

        for i in range(1, n_g):
            w_group(b, i).start()
        if b == 0:
            for buf, ss, rs in ((x_all, xs, xr),):
                for i in range(1, n_x):
                    arrival(buf, ss, rs, ((xx + i) % n_x) * 2 + core).wait_recv()
                    relay_copy(buf, ss, rs, i).start()

    for i in range(1, n_x):
        arrival(u_all, us, ur, ((xx + i) % n_x) * 2 + core).wait_recv()
        relay_copy(u_all, us, ur, i).start()
    for buf, ss, rs in ((x_all, xs, xr), (u_all, us, ur)):
        arrival(buf, ss, rs, partner).wait_recv()
        for i in range(1, n_x):
            arrival(buf, ss, rs, ((xx + i) % n_x) * 2 + 1 - core).wait_recv()
    for i in range(1, n_t):
        j = (hh + n_t - i) % n_t
        rc(k_all.at[j], k_all.at[j], ks.at[i - 1], kr.at[j], member(partner)).wait_recv()
    for i in range(1, n_g):
        for b in range(n_t):
            w_group_arrival(b, i).wait_recv()

    score_scale = 1.0 / HEAD**0.5
    lane = lax.broadcasted_iota(jnp.int32, (1, hw), 1)

    def gn_copy(j, i):
        return rc(gn_send.at[arow(j)], gn_recv.at[arow(hh)], gns.at[i], gnr.at[hh], member(j))

    def attend(i, carry):
        j = (hh + 1 + i) % n_t
        own = arow(j)
        projected = mm(x_all[own, :], w_all[:, : 3 * hw]).astype(BF16)
        g_att = mm(u_all[own, :], w_all[:, 3 * hw :]).astype(BF16)
        query, keys, value = projected[:, :hw], projected[:, hw : 2 * hw], projected[:, 2 * hw :]
        q_image = image_of(lax.broadcasted_iota(jnp.int32, (rows, 1), 0), images).astype(F32)
        allowed = q_image == k_all[j][0:1, :rows]
        zero = jnp.zeros((rows, hw), F32)
        att, dq, dk, dv = zero, zero, zero, zero
        for h in range(heads):
            here = jnp.where(jnp.logical_and(lane >= h * HEAD, lane < (h + 1) * HEAD), 1.0, 0.0).astype(BF16)
            qh = query * here
            gh = g_att * here
            scores = jnp.where(allowed, mm_nt(qh, keys) * score_scale, -1e30)
            top = jnp.max(scores, axis=-1, keepdims=True)
            weight = jnp.exp(scores - top)
            probs = weight * (1.0 / jnp.sum(weight, axis=-1, keepdims=True))
            probs_low = probs.astype(BF16)
            att += mm(probs_low, value * here)
            g_probs = mm_nt(gh, value)
            delta = jnp.sum(probs * g_probs, axis=-1, keepdims=True)
            g_scores = (probs * (g_probs - delta) * score_scale).astype(BF16)
            dv += mm_tn(probs_low, gh)
            dq += mm(g_scores, keys * here)
            dk += mm_tn(g_scores, qh)
        att_all[own, :] = att.astype(BF16)
        gp_all[own, :hw] = dq.astype(BF16)
        gp_all[own, hw : 2 * hw] = dk.astype(BF16)
        gp_all[own, 2 * hw :] = dv.astype(BF16)
        part = mm_nt(gp_all[own, :], w_all[:, : 3 * hw]).astype(BF16)

        @pl.when(i < n_t - 1)
        def _():
            gn_send[own, :] = part
            gn_copy(j, i).start()

        @pl.when(i == n_t - 1)
        def _():
            gn_recv[arow(hh), :] = part

        return carry

    lax.fori_loop(0, n_t, attend, 0)

    half = width // n_g
    chunk = min(256, half)

    def g_copy(b, i):
        k = (i - 1) * n_t + b
        other = (g + i) % n_g
        return rc(
            g_send.at[wrow(other, b)], g_recv.at[pl.ds(k * wrows, wrows)], ggs.at[k], ggr.at[k],
            (other * n_t + hh, z),
        )

    for i in list(range(1, n_g)) + [0]:
        other = (g + i) % n_g
        for part in range(half // chunk):
            span = pl.ds(pl.multiple_of(other * half + part * chunk, 128), chunk)
            g_send[span, : 3 * hw] = mm_tn(x_all[:, span], gp_all[...]).astype(BF16)
            g_send[span, 3 * hw :] = mm_tn(u_all[:, span], att_all[...]).astype(BF16)
            if i:
                for b in range(n_t):
                    if (b + 1) * wrows <= (part + 1) * chunk and (b + 1) * wrows > part * chunk:
                        g_copy(b, i).start()

    for i in range(1, n_t):
        j = (hh + n_t - i) % n_t
        rc(gn_recv.at[arow(j)], gn_recv.at[arow(j)], gns.at[0], gnr.at[j], member(partner)).wait_recv()
    g_normed = gn_recv[pl.ds(0, rows), :].astype(F32)
    for j in range(1, n_t):
        g_normed = g_normed + gn_recv[pl.ds(j * rows, rows), :].astype(F32)
    scaled = xhat[...]
    a_buf[hh, 0:1, :] = jnp.sum(g_normed * scaled, axis=0, keepdims=True)
    a_buf[hh, 1:2, :] = jnp.sum(g_normed, axis=0, keepdims=True)

    def a_copy(i):
        return rc(a_buf.at[hh], a_buf.at[hh], a_s.at[i - 1], a_r.at[hh], member((hh + i) % n_t))

    def b_copy(i):
        return rc(b_buf.at[z], b_buf.at[z], b_s.at[i - 1], b_r.at[z], (dp, (z + i) % n_t))

    def c_copy(i):
        return rc(c_buf.at[g], c_buf.at[g], c_s.at[i - 1], c_r.at[g], (((g + i) % n_g) * n_t + hh, z))

    for i in range(1, n_t):
        a_copy(i).start()
    g_scaled = g_normed * gain[...]
    g_ln = rstd_s[...] * (
        g_scaled
        - jnp.mean(g_scaled, axis=-1, keepdims=True)
        - scaled * jnp.mean(g_scaled * scaled, axis=-1, keepdims=True)
    )
    packed = (u_all[arow(hh), :].astype(F32) + g_ln).astype(BF16)
    gt_ref[...] = mm_tn(packing(rows, local_rows, images), packed).astype(BF16)
    for i in range(1, n_t):
        j = (hh + n_t - i) % n_t
        rc(a_buf.at[j], a_buf.at[j], a_s.at[0], a_r.at[j], member(partner)).wait_recv()
    total = a_buf[0]
    for j in range(1, n_t):
        total = total + a_buf[j]
    b_buf[z] = total
    for i in range(1, n_t):
        b_copy(i).start()

    def zrow(b):
        return pl.ds(b * wrows, wrows)

    def z_up_copy(b):
        return rc(z_send.at[zrow(b)], z_down.at[zrow(b)], gzs.at[b], gdr.at[b], next_up)

    def z_down_copy(b):
        return rc(z_send.at[zrow(b)], z_up.at[zrow(b)], gzs.at[b], gur.at[b], next_down)

    def final_copy(b):
        return rc(z_send.at[zrow(b)], fin, fs.at[b], fr, member(b))

    for b in range(n_t):
        total = g_send[wrow(g, b), :].astype(F32)
        for i in range(1, n_g):
            k = (i - 1) * n_t + b
            g_copy(b, i).wait_recv()
            total = total + g_recv[pl.ds(k * wrows, wrows), :].astype(F32)
        acc_s[...] = total

        @pl.when(go_up)
        def _():
            rc(z_up.at[zrow(b)], z_up.at[zrow(b)], gzs.at[b], gur.at[b], next_up).wait_recv()
            acc_s[...] += z_up[zrow(b), :].astype(F32)

        @pl.when(go_down)
        def _():
            rc(z_down.at[zrow(b)], z_down.at[zrow(b)], gzs.at[b], gdr.at[b], next_down).wait_recv()
            acc_s[...] += z_down[zrow(b), :].astype(F32)

        z_send[zrow(b), :] = acc_s[...].astype(BF16)

        @pl.when(z > hh)
        def _():
            z_down_copy(b).start()

        @pl.when(z < hh)
        def _():
            z_up_copy(b).start()

        @pl.when(jnp.logical_and(is_root, hh != b))
        def _():
            final_copy(b).start()

        @pl.when(jnp.logical_and(is_root, hh == b))
        def _():
            gw_ref[...] = acc_s[...]

        if b == 0:
            for i in range(1, n_t):
                j = (z + n_t - i) % n_t
                rc(b_buf.at[j], b_buf.at[j], b_s.at[0], b_r.at[j], next_up).wait_recv()
            total = b_buf[0]
            for j in range(1, n_t):
                total = total + b_buf[j]
            c_buf[g] = total
            for i in range(1, n_g):
                c_copy(i).start()

    for i in range(1, n_g):
        j = (g + n_g - i) % n_g
        rc(c_buf.at[j], c_buf.at[j], c_s.at[0], c_r.at[j], (((g + i) % n_g) * n_t + hh, z)).wait_recv()
    total = c_buf[0]
    for j in range(1, n_g):
        total = total + c_buf[j]
    gb_ref[...] = total

    @pl.when(jnp.logical_not(is_root))
    def _():
        rc(fin, fin, fs.at[0], fr, member(partner)).wait_recv()
        gw_ref[...] = fin[...].astype(F32)

    @pl.when(jnp.logical_not(is_root))
    def _():
        w_first().wait_send()

    for i in range(1, n_t):
        k_copy(i).wait_send()
        a_copy(i).wait_send()
        b_copy(i).wait_send()
        gn_copy((hh + i) % n_t, i - 1).wait_send()
    for buf, ss, rs in ((x_all, xs, xr), (u_all, us, ur)):
        for i in range(n_x):
            own_copy(buf, ss, rs, i).wait_send()
        for i in range(1, n_x):
            relay_copy(buf, ss, rs, i).wait_send()
    for b in range(n_t):

        @pl.when(go_up)
        def _():
            w_up(b).wait_send()

        @pl.when(go_down)
        def _():
            w_down(b).wait_send()

        for i in range(1, n_g):
            w_group(b, i).wait_send()
            g_copy(b, i).wait_send()

        @pl.when(jnp.logical_not(is_root))
        def _():
            z_up_copy(b).wait_send()

        @pl.when(jnp.logical_and(is_root, hh != b))
        def _():
            final_copy(b).wait_send()

    for i in range(1, n_g):
        c_copy(i).wait_send()


def on_device(n_dp, n_t, tokens, upstream, counts, norm_gain, norm_bias, w_qkv, w_out):
    local_rows, width = tokens.shape
    n_g = n_dp // n_t
    n_x = n_t // 2
    wrows = w_qkv.shape[0]
    hw = w_out.shape[0]
    heads = hw // HEAD
    cols = 4 * hw
    rows = -(-(local_rows // CAP * MAXC) // 16) * 16
    lanes = -(-rows // 128) * 128
    by_kind = w_qkv.reshape(wrows, heads, 3, HEAD).transpose(0, 2, 1, 3).reshape(wrows, 3 * hw)
    wblk = jnp.concatenate([by_kind, w_out.T], axis=1)
    vmem = pl.BlockSpec(memory_space=pltpu.VMEM)
    dma = pltpu.SemaphoreType.DMA
    others = max(n_g - 1, 1)
    grad_tokens, grad_w, grad_gb = pl.pallas_call(
        functools.partial(kernel, n_dp, n_t),
        out_shape=(
            jax.ShapeDtypeStruct((local_rows, width), BF16),
            jax.ShapeDtypeStruct((wrows, cols), F32),
            jax.ShapeDtypeStruct((2, width), F32),
        ),
        in_specs=[pl.BlockSpec(memory_space=pltpu.SMEM)] + [vmem] * 5,
        out_specs=(vmem, vmem, vmem),
        scratch_shapes=[
            pltpu.VMEM((n_t * rows, width), BF16),
            pltpu.VMEM((n_t * rows, width), BF16),
            pltpu.VMEM((n_t, 8, lanes), F32),
            pltpu.VMEM((width, cols), BF16),
            pltpu.VMEM((rows, width), F32),
            pltpu.VMEM((rows, 1), F32),
            pltpu.VMEM((n_t * rows, 3 * hw), BF16),
            pltpu.VMEM((n_t * rows, hw), BF16),
            pltpu.VMEM((n_t * rows, width), BF16),
            pltpu.VMEM((n_t * rows, width), BF16),
            pltpu.VMEM((width, cols), BF16),
            pltpu.VMEM((others * n_t * wrows, cols), BF16),
            pltpu.VMEM((n_t * wrows, cols), BF16),
            pltpu.VMEM((n_t * wrows, cols), BF16),
            pltpu.VMEM((n_t * wrows, cols), BF16),
            pltpu.VMEM((wrows, cols), F32),
            pltpu.VMEM((wrows, cols), BF16),
            pltpu.VMEM((n_t, 2, width), F32),
            pltpu.VMEM((n_t, 2, width), F32),
            pltpu.VMEM((n_g, 2, width), F32),
            dma((2 * n_x,)), dma((n_t,)), dma((2 * n_x,)), dma((n_t,)),
            dma((n_t,)), dma((n_t,)),
            dma, dma((n_t,)), dma((n_t,)), dma((n_t,)), dma((n_t,)),
            dma((others * n_t,)), dma((others * n_t,)),
            dma((n_t,)), dma((n_t,)),
            dma((others * n_t,)), dma((others * n_t,)),
            dma((n_t,)), dma((n_t,)), dma((n_t,)), dma((n_t,)), dma,
            dma((n_t,)), dma((n_t,)), dma((n_t,)), dma((n_t,)), dma((n_t,)), dma((n_t,)),
        ],
        compiler_params=pltpu.CompilerParams(
            collective_id=0, has_side_effects=True, vmem_limit_bytes=56 << 20
        ),
    )(counts, tokens, upstream, norm_gain.reshape(1, -1), norm_bias.reshape(1, -1), wblk)
    grad_qkv = (
        grad_w[:, : 3 * hw].reshape(wrows, 3, heads, HEAD).transpose(0, 2, 1, 3).reshape(wrows, 3 * hw)
    )
    return (grad_tokens, grad_qkv, grad_w[:, 3 * hw :].T, grad_gb[0], grad_gb[1])


def solution(mesh):
    return jax.shard_map(
        functools.partial(on_device, mesh.shape["dp"], mesh.shape["tensor"]),
        mesh=mesh,
        in_specs=(
            P(("dp", "tensor"), None),
            P(("dp", "tensor"), None),
            P("dp"),
            P(),
            P(),
            P("dp", "tensor"),
            P("tensor", "dp"),
        ),
        out_specs=(P(("dp", "tensor"), None), P("dp", "tensor"), P("tensor", "dp"), P(), P()),
        check_vma=False,
    )
```

time: 333 us -> 133 us (0.40)
  waiting for transfers between devices: 182 us -> 0 us
  Pallas kernels: 0 us -> 123 us
  blocking collectives: 52.1 us -> 0 us
  matrix products: 41.2 us -> 0 us
  local copies, waits for them, and re-layouts: 29 us -> 8.15 us
  between operations: 14.3 us -> 0.69 us
  other arithmetic: 13.4 us -> 0.73 us
    pallas_call x0 -> x1, Pallas kernels: none -> 123 us  [on_device(): pl.pallas_call(functools.partial(kernel, n_dp, n_t), out_shape=(jax.Shape...]
    all_gather x3 -> x0, waiting for transfers between devices: 86.4 us -> none  [the longest x1 47.8 us: on_device(): all_normed = lax.all_gather(normed, 'tensor', axis=0, tiled=True)]
    reduce_scatter x2 -> x0, waiting for transfers between devices: 84 us -> none  [the longest x1 44.1 us: on_device(): lax.psum_scatter(lax.dot_general(grad_proj, qkv_cols, (((1,), (1,)), ((),...]
    psum x1 -> x0, blocking collectives: 39.5 us -> none  [on_device(): lax.psum((jnp.sum(grad_normed * scaled, axis=0), jnp.sum(grad_normed, axi...]
    dot_general x10 -> x0, matrix products: 36.4 us -> none  [the longest x1 6.07 us: on_device(): jnp.einsum('bhqk,bkhe->bqhe', grad_scores, key_rows, preferred_element_ty...]
    all_gather x1 -> x0, blocking collectives: 12.6 us -> none  [on_device(): out_rows = lax.all_gather(w_out, 'dp', axis=1, tiled=True)]
    reshape x5 -> x1, local copies, waits for them, and re-layouts: 12.3 us -> 0.15 us  [on_device(): w_qkv.reshape(wrows, heads, 3, HEAD).transpose(0, 2, 1, 3)]
    unnamed x7 -> x0, waiting for transfers between devices: 12 us -> none
  transfers between devices with their start and end apart: 6 -> 0, of which waited for: 6 -> 0; matrix products, arithmetic and copies ran while one was open for 15% -> 0% of each run, Pallas kernels for 0% -> 0%
where the time goes in v1:
time: 133 us; the launch traced here: 132 us
  Pallas kernels  123 us (92%)
  local copies, waits for them, and re-layouts  8.15 us (6%)
    pallas_call x1, Pallas kernels, on_device(): pl.pallas_call(functools.partial(kernel, n_dp, n_t), out_shape=(jax.Shape...  123 us
    unnamed x7, local copies, waits for them, and re-layouts  4.49 us

profile of v1, /device:TPU:0, one launch (start us, length us, event | category | flops | bytes accessed | tf_op | source)
XLA Modules:
  0.0 132.2 jit_solution(8734772308065798343)
XLA Ops:
  0.6 0.9 copy.18
  1.6 1.1 copy.16
  2.7 0.1 copy.19
  2.8 0.7 pad_maximum_fusion.wblk
  3.6 122.6 %shard_map.110 = (bf16[256,1024]{1,0:T(8,128)(2,1)}, f32[128,1024]{1,0:T(8,128)}, f32[2,1024]{1,0:T(2,128)}) custom-call(s32[16]{0:T(128)} %counts.1, bf16[256,1024]{1,0:T(8,128)(2,1)} %tokens.1, bf16[256,1024]{1,0:T(8,128)(2,1)} %upstream.1, f32[1,1024]{1,0:T(1,128)} %bitcast.20, f32[1,1024]{1,0:T(1,128)} %bitcast.21, bf16[128,1024]{1,0:T(8,128)(2,1)} %pad_maximum_fusion.wblk), custom_call_target="tpu_custom_call" | custom-call | tf_op jit(solution)/shard_map/pallas_call | solution.py:456
  126.2 1.4 %fusion = (f32[1,1024]{1,0:T(1,128)}, f32[1,1024]{1,0:T(1,128)}) fusion(f32[2,1024]{1,0:T(2,128)} %get-tuple-element.10), kind=kLoop, calls=%fused_computation.2 | loop fusion | bytes 16384 | tf_op jit(solution)/shard_map/slice | solution.py:502
  127.6 0.9 slice_bitcast_fusion
  128.5 1.0 slice.12
  129.5 0.2 copy.20
  129.7 0.0 copy-start
  129.7 0.9 copy.22
  130.7 0.8 copy.23
  131.4 0.0 copy-done
  131.4 0.8 copy.25
  (2 shorter events, 0.0 us)
Async XLA Ops:
  129.7 1.7 %copy-start = (bf16[256,1024]{1,0:T(8,128)(2,1)S(1)}, bf16[256,1024]{1,0:T(8,128)(2,1)}, u32[]{:S(2)}) copy-start(bf16[256,1024]{1,0:T(8,128)(2,1)} %get-tuple-element.28) | copy-start | bytes 1572868

commit v2 on v1

--- a/solution.py
+++ b/solution.py
@@ -9,6 +9,7 @@
 
 HEAD = 64
 CAP = 64
+SPLIT = 4
 MAXC = 49
 F32 = jnp.float32
 BF16 = jnp.bfloat16
@@ -74,8 +75,16 @@
     def member(h):
         return (g * n_t + h, z)
 
-    def wrow(gi, b):
-        return pl.ds(pl.multiple_of((gi * n_t + b) * wrows, wrows), wrows)
+    prow = wrows // SPLIT
+    pieces = n_t * SPLIT
+
+    def wrow(gi, p):
+        return pl.ds(pl.multiple_of((gi * pieces + p) * prow, prow), prow)
+
+    def near(k):
+        return ((xx + k // (2 * SPLIT)) % n_x) * 2 + (core + (k // SPLIT) % 2) % 2
+
+    order = [(near(k), near(k) * SPLIT + k % SPLIT, k) for k in range(pieces)]
 
     def arow(j):
         return pl.ds(pl.multiple_of(j * rows, 16), rows)
@@ -96,16 +105,19 @@
     next_up = (dp, (z + 1) % n_t)
     next_down = (dp, (z + n_t - 1) % n_t)
 
-    def w_first():
-        return rc(wblk, w_all.at[wrow(g, hh)], w1s, w1r.at[hh], member(z))
-
-    @pl.when(jnp.logical_not(is_root))
-    def _():
-        w_first().start()
-
-    @pl.when(is_root)
-    def _():
-        w_all[wrow(g, hh), :] = wblk[...]
+    def w_first(s):
+        p = hh * SPLIT + s
+        return rc(wblk.at[pl.ds(s * prow, prow)], w_all.at[wrow(g, p)], w1s.at[s], w1r.at[p], member(z))
+
+    for s in range(SPLIT):
+
+        @pl.when(jnp.logical_not(is_root))
+        def _():
+            w_first(s).start()
+
+        @pl.when(is_root)
+        def _():
+            w_all[wrow(g, hh * SPLIT + s), :] = wblk[pl.ds(s * prow, prow), :]
 
     select = packing(rows, local_rows, images)
     row = lax.broadcasted_iota(jnp.int32, (rows, 1), 0)
@@ -162,47 +174,44 @@
         return rc(w_all.at[wrow(g, b)], w_all.at[wrow(g, b)], wds.at[b], wzr.at[b], next_down)
 
     def w_group(b, i):
-        k = (i - 1) * n_t + b
+        k = (i - 1) * pieces + b
         return rc(
             w_all.at[wrow(g, b)], w_all.at[wrow(g, b)], wgs.at[k], wgr.at[k],
             (((g + i) % n_g) * n_t + hh, z),
         )
 
     def w_group_arrival(b, i):
-        k = (i - 1) * n_t + b
+        k = (i - 1) * pieces + b
         src = w_all.at[wrow((g + n_g - i) % n_g, b)]
         return rc(src, src, wgs.at[k], wgr.at[k], (((g + i) % n_g) * n_t + hh, z))
 
-    for b in range(n_t):
-        block = w_all.at[wrow(g, b)]
+    for b, p, k in order:
+        block = w_all.at[wrow(g, p)]
 
         @pl.when(jnp.logical_and(is_root, hh != b))
         def _():
-            rc(block, block, w1s, w1r.at[b], member(partner)).wait_recv()
+            rc(block, block, w1s.at[0], w1r.at[p], member(partner)).wait_recv()
 
         @pl.when(jnp.logical_not(is_root))
         def _():
-            rc(block, block, wus.at[b], wzr.at[b], next_up).wait_recv()
+            rc(block, block, wus.at[p], wzr.at[p], next_up).wait_recv()
 
         @pl.when(go_up)
         def _():
-            w_up(b).start()
+            w_up(p).start()
 
         @pl.when(go_down)
         def _():
-            w_down(b).start()
+            w_down(p).start()
 
         for i in range(1, n_g):
-            w_group(b, i).start()
-        if b == 0:
-            for buf, ss, rs in ((x_all, xs, xr),):
+            w_group(p, i).start()
+        for buf, ss, rs, when in ((x_all, xs, xr, pieces // 2 + 1), (u_all, us, ur, pieces - 1)):
+            if k == when:
                 for i in range(1, n_x):
                     arrival(buf, ss, rs, ((xx + i) % n_x) * 2 + core).wait_recv()
                     relay_copy(buf, ss, rs, i).start()
 
-    for i in range(1, n_x):
-        arrival(u_all, us, ur, ((xx + i) % n_x) * 2 + core).wait_recv()
-        relay_copy(u_all, us, ur, i).start()
     for buf, ss, rs in ((x_all, xs, xr), (u_all, us, ur)):
         arrival(buf, ss, rs, partner).wait_recv()
         for i in range(1, n_x):
@@ -211,8 +220,8 @@
         j = (hh + n_t - i) % n_t
         rc(k_all.at[j], k_all.at[j], ks.at[i - 1], kr.at[j], member(partner)).wait_recv()
     for i in range(1, n_g):
-        for b in range(n_t):
-            w_group_arrival(b, i).wait_recv()
+        for b, p, k in order:
+            w_group_arrival(p, i).wait_recv()
 
     score_scale = 1.0 / HEAD**0.5
     lane = lax.broadcasted_iota(jnp.int32, (1, hw), 1)
@@ -269,10 +278,10 @@
     chunk = min(256, half)
 
     def g_copy(b, i):
-        k = (i - 1) * n_t + b
+        k = (i - 1) * pieces + b
         other = (g + i) % n_g
         return rc(
-            g_send.at[wrow(other, b)], g_recv.at[pl.ds(k * wrows, wrows)], ggs.at[k], ggr.at[k],
+            g_send.at[wrow(other, b)], g_recv.at[pl.ds(pl.multiple_of(k * prow, prow), prow)], ggs.at[k], ggr.at[k],
             (other * n_t + hh, z),
         )
 
@@ -282,20 +291,9 @@
             span = pl.ds(pl.multiple_of(other * half + part * chunk, 128), chunk)
             g_send[span, : 3 * hw] = mm_tn(x_all[:, span], gp_all[...]).astype(BF16)
             g_send[span, 3 * hw :] = mm_tn(u_all[:, span], att_all[...]).astype(BF16)
-            if i:
-                for b in range(n_t):
-                    if (b + 1) * wrows <= (part + 1) * chunk and (b + 1) * wrows > part * chunk:
-                        g_copy(b, i).start()
-
-    for i in range(1, n_t):
-        j = (hh + n_t - i) % n_t
-        rc(gn_recv.at[arow(j)], gn_recv.at[arow(j)], gns.at[0], gnr.at[j], member(partner)).wait_recv()
-    g_normed = gn_recv[pl.ds(0, rows), :].astype(F32)
-    for j in range(1, n_t):
-        g_normed = g_normed + gn_recv[pl.ds(j * rows, rows), :].astype(F32)
-    scaled = xhat[...]
-    a_buf[hh, 0:1, :] = jnp.sum(g_normed * scaled, axis=0, keepdims=True)
-    a_buf[hh, 1:2, :] = jnp.sum(g_normed, axis=0, keepdims=True)
+        if i:
+            for b, p, k in order[::-1]:
+                g_copy(p, i).start()
 
     def a_copy(i):
         return rc(a_buf.at[hh], a_buf.at[hh], a_s.at[i - 1], a_r.at[hh], member((hh + i) % n_t))
@@ -306,28 +304,40 @@
     def c_copy(i):
         return rc(c_buf.at[g], c_buf.at[g], c_s.at[i - 1], c_r.at[g], (((g + i) % n_g) * n_t + hh, z))
 
-    for i in range(1, n_t):
-        a_copy(i).start()
-    g_scaled = g_normed * gain[...]
-    g_ln = rstd_s[...] * (
-        g_scaled
-        - jnp.mean(g_scaled, axis=-1, keepdims=True)
-        - scaled * jnp.mean(g_scaled * scaled, axis=-1, keepdims=True)
-    )
-    packed = (u_all[arow(hh), :].astype(F32) + g_ln).astype(BF16)
-    gt_ref[...] = mm_tn(packing(rows, local_rows, images), packed).astype(BF16)
-    for i in range(1, n_t):
-        j = (hh + n_t - i) % n_t
-        rc(a_buf.at[j], a_buf.at[j], a_s.at[0], a_r.at[j], member(partner)).wait_recv()
-    total = a_buf[0]
-    for j in range(1, n_t):
-        total = total + a_buf[j]
-    b_buf[z] = total
-    for i in range(1, n_t):
-        b_copy(i).start()
+    def finish_tokens():
+        for i in range(1, n_t):
+            j = (hh + n_t - i) % n_t
+            rc(gn_recv.at[arow(j)], gn_recv.at[arow(j)], gns.at[0], gnr.at[j], member(partner)).wait_recv()
+        g_normed = gn_recv[pl.ds(0, rows), :].astype(F32)
+        for j in range(1, n_t):
+            g_normed = g_normed + gn_recv[pl.ds(j * rows, rows), :].astype(F32)
+        scaled = xhat[...]
+        a_buf[hh, 0:1, :] = jnp.sum(g_normed * scaled, axis=0, keepdims=True)
+        a_buf[hh, 1:2, :] = jnp.sum(g_normed, axis=0, keepdims=True)
+        for i in range(1, n_t):
+            a_copy(i).start()
+        g_scaled = g_normed * gain[...]
+        g_ln = rstd_s[...] * (
+            g_scaled
+            - jnp.mean(g_scaled, axis=-1, keepdims=True)
+            - scaled * jnp.mean(g_scaled * scaled, axis=-1, keepdims=True)
+        )
+        packed = (u_all[arow(hh), :].astype(F32) + g_ln).astype(BF16)
+        gt_ref[...] = mm_tn(packing(rows, local_rows, images), packed).astype(BF16)
+
+    def reduce_first():
+        for i in range(1, n_t):
+            j = (hh + n_t - i) % n_t
+            rc(a_buf.at[j], a_buf.at[j], a_s.at[0], a_r.at[j], member(partner)).wait_recv()
+        total = a_buf[0]
+        for j in range(1, n_t):
+            total = total + a_buf[j]
+        b_buf[z] = total
+        for i in range(1, n_t):
+            b_copy(i).start()
 
     def zrow(b):
-        return pl.ds(b * wrows, wrows)
+        return pl.ds(pl.multiple_of(b * prow, prow), prow)
 
     def z_up_copy(b):
         return rc(z_send.at[zrow(b)], z_down.at[zrow(b)], gzs.at[b], gdr.at[b], next_up)
@@ -336,14 +346,17 @@
         return rc(z_send.at[zrow(b)], z_up.at[zrow(b)], gzs.at[b], gur.at[b], next_down)
 
     def final_copy(b):
-        return rc(z_send.at[zrow(b)], fin, fs.at[b], fr, member(b))
-
-    for b in range(n_t):
+        part = b % SPLIT
+        return rc(
+            z_send.at[zrow(b)], fin.at[zrow(part)], fs.at[b], fr.at[part], member(b // SPLIT)
+        )
+
+    for head, b, step in order[::-1]:
         total = g_send[wrow(g, b), :].astype(F32)
         for i in range(1, n_g):
-            k = (i - 1) * n_t + b
+            k = (i - 1) * pieces + b
             g_copy(b, i).wait_recv()
-            total = total + g_recv[pl.ds(k * wrows, wrows), :].astype(F32)
+            total = total + g_recv[pl.ds(pl.multiple_of(k * prow, prow), prow), :].astype(F32)
         acc_s[...] = total
 
         @pl.when(go_up)
@@ -366,24 +379,28 @@
         def _():
             z_up_copy(b).start()
 
-        @pl.when(jnp.logical_and(is_root, hh != b))
+        @pl.when(jnp.logical_and(is_root, hh != head))
         def _():
             final_copy(b).start()
 
-        @pl.when(jnp.logical_and(is_root, hh == b))
-        def _():
-            gw_ref[...] = acc_s[...]
-
-        if b == 0:
-            for i in range(1, n_t):
-                j = (z + n_t - i) % n_t
-                rc(b_buf.at[j], b_buf.at[j], b_s.at[0], b_r.at[j], next_up).wait_recv()
-            total = b_buf[0]
-            for j in range(1, n_t):
-                total = total + b_buf[j]
-            c_buf[g] = total
-            for i in range(1, n_g):
-                c_copy(i).start()
+        @pl.when(jnp.logical_and(is_root, hh == head))
+        def _():
+            gw_ref[pl.ds((step % SPLIT) * prow, prow), :] = acc_s[...]
+
+        if step == pieces // 2 - 1:
+            finish_tokens()
+        if step == min(1, pieces - 1):
+            reduce_first()
+
+    for i in range(1, n_t):
+        j = (z + n_t - i) % n_t
+        rc(b_buf.at[j], b_buf.at[j], b_s.at[0], b_r.at[j], next_up).wait_recv()
+    total = b_buf[0]
+    for j in range(1, n_t):
+        total = total + b_buf[j]
+    c_buf[g] = total
+    for i in range(1, n_g):
+        c_copy(i).start()
 
     for i in range(1, n_g):
         j = (g + n_g - i) % n_g
@@ -395,12 +412,15 @@
 
     @pl.when(jnp.logical_not(is_root))
     def _():
-        rc(fin, fin, fs.at[0], fr, member(partner)).wait_recv()
+        for part in range(SPLIT):
+            piece = fin.at[zrow(part)]
+            rc(piece, piece, fs.at[part], fr.at[part], member(partner)).wait_recv()
         gw_ref[...] = fin[...].astype(F32)
 
     @pl.when(jnp.logical_not(is_root))
     def _():
-        w_first().wait_send()
+        for s in range(SPLIT):
+            w_first(s).wait_send()
 
     for i in range(1, n_t):
         k_copy(i).wait_send()
@@ -412,7 +432,7 @@
             own_copy(buf, ss, rs, i).wait_send()
         for i in range(1, n_x):
             relay_copy(buf, ss, rs, i).wait_send()
-    for b in range(n_t):
+    for head, b, step in order:
 
         @pl.when(go_up)
         def _():
@@ -430,7 +450,7 @@
         def _():
             z_up_copy(b).wait_send()
 
-        @pl.when(jnp.logical_and(is_root, hh != b))
+        @pl.when(jnp.logical_and(is_root, hh != head))
         def _():
             final_copy(b).wait_send()
 
@@ -453,6 +473,7 @@
     vmem = pl.BlockSpec(memory_space=pltpu.VMEM)
     dma = pltpu.SemaphoreType.DMA
     others = max(n_g - 1, 1)
+    pieces = n_t * SPLIT
     grad_tokens, grad_w, grad_gb = pl.pallas_call(
         functools.partial(kernel, n_dp, n_t),
         out_shape=(
@@ -478,18 +499,18 @@
             pltpu.VMEM((n_t * wrows, cols), BF16),
             pltpu.VMEM((n_t * wrows, cols), BF16),
             pltpu.VMEM((n_t * wrows, cols), BF16),
-            pltpu.VMEM((wrows, cols), F32),
+            pltpu.VMEM((wrows // SPLIT, cols), F32),
             pltpu.VMEM((wrows, cols), BF16),
             pltpu.VMEM((n_t, 2, width), F32),
             pltpu.VMEM((n_t, 2, width), F32),
             pltpu.VMEM((n_g, 2, width), F32),
             dma((2 * n_x,)), dma((n_t,)), dma((2 * n_x,)), dma((n_t,)),
             dma((n_t,)), dma((n_t,)),
-            dma, dma((n_t,)), dma((n_t,)), dma((n_t,)), dma((n_t,)),
-            dma((others * n_t,)), dma((others * n_t,)),
+            dma((SPLIT,)), dma((pieces,)), dma((pieces,)), dma((pieces,)), dma((pieces,)),
+            dma((others * pieces,)), dma((others * pieces,)),
             dma((n_t,)), dma((n_t,)),
-            dma((others * n_t,)), dma((others * n_t,)),
-            dma((n_t,)), dma((n_t,)), dma((n_t,)), dma((n_t,)), dma,
+            dma((others * pieces,)), dma((others * pieces,)),
+            dma((pieces,)), dma((pieces,)), dma((pieces,)), dma((pieces,)), dma((SPLIT,)),
             dma((n_t,)), dma((n_t,)), dma((n_t,)), dma((n_t,)), dma((n_t,)), dma((n_t,)),
         ],
         compiler_params=pltpu.CompilerParams(

time: 133 us -> 106 us (0.80)
  Pallas kernels: 123 us -> 96.2 us
    pallas_call x1, Pallas kernels: 123 us -> 96.2 us  [on_device(): pl.pallas_call(functools.partial(kernel, n_dp, n_t), out_shape=(jax.Shape...]
where the time goes in v2:
time: 106 us
  Pallas kernels  96.2 us (91%)
  local copies, waits for them, and re-layouts  8.15 us (8%)
    pallas_call x1, Pallas kernels, on_device(): pl.pallas_call(functools.partial(kernel, n_dp, n_t), out_shape=(jax.Shape...  96.2 us
    unnamed x7, local copies, waits for them, and re-layouts  4.49 us

profile of v2, /device:TPU:0, one launch (start us, length us, event | category | flops | bytes accessed | tf_op | source)
XLA Modules:
  0.0 105.7 jit_solution(8785277923719631659)
XLA Ops:
  0.6 0.9 copy.18
  1.6 1.1 %copy.16 = bf16[128,768]{0,1:T(8,128)(2,1)S(1)} copy(bf16[128,768]{1,0:T(8,128)(2,1)} %param.12) | data formatting | bytes 393216 | tf_op args[5]
  2.7 0.1 copy.19
  2.8 0.7 pad_maximum_fusion.wblk
  3.6 96.2 %shard_map.110 = (bf16[256,1024]{1,0:T(8,128)(2,1)}, f32[128,1024]{1,0:T(8,128)}, f32[2,1024]{1,0:T(2,128)}) custom-call(s32[16]{0:T(128)} %counts.1, bf16[256,1024]{1,0:T(8,128)(2,1)} %tokens.1, bf16[256,1024]{1,0:T(8,128)(2,1)} %upstream.1, f32[1,1024]{1,0:T(1,128)} %bitcast.20, f32[1,1024]{1,0:T(1,128)} %bitcast.21, bf16[128,1024]{1,0:T(8,128)(2,1)} %pad_maximum_fusion.wblk), custom_call_target="tpu_custom_call" | custom-call | tf_op jit(solution)/shard_map/pallas_call | solution.py:477
  99.8 1.4 %fusion = (f32[1,1024]{1,0:T(1,128)}, f32[1,1024]{1,0:T(1,128)}) fusion(f32[2,1024]{1,0:T(2,128)} %get-tuple-element.10), kind=kLoop, calls=%fused_computation.2 | loop fusion | bytes 16384 | tf_op jit(solution)/shard_map/slice | solution.py:523
  101.1 0.9 slice_bitcast_fusion
  102.0 1.0 slice.12
  103.1 0.2 copy.20
  103.3 0.0 copy-start
  103.3 0.9 copy.22
  104.2 0.8 copy.23
  105.0 0.0 copy-done
  105.0 0.8 copy.25
  (2 shorter events, 0.0 us)
Async XLA Ops:
  103.3 1.7 %copy-start = (bf16[256,1024]{1,0:T(8,128)(2,1)S(1)}, bf16[256,1024]{1,0:T(8,128)(2,1)}, u32[]{:S(2)}) copy-start(bf16[256,1024]{1,0:T(8,128)(2,1)} %get-tuple-element.28) | copy-start | bytes 1572868
